TPU v7x, 32 devices: a whole 2x2x4 slice. The times are simulated.
32 devices in a mesh: cells: 8 (over z, x), genes: 4 (over y, core).
Axes of the slice: x: 2, y: 2, z: 4, core: 2. Of those that a mesh axis runs over, the one named last changes fastest.
Arguments:
- counts: int32 [38912, 4000], P('cells', 'genes'), may hold values from 0 to 674, as said below
- sketch: bfloat16 [4000, 128], P('genes'), may hold values from -6 to 6
Outputs:
- basis: float32 [38912, 128], P('cells')
- loadings: float32 [4000, 128], P('genes')
Inputs may be any that keep to these rules, and one draw needn't show every extreme that they name: `counts`: every cell and every gene has a positive total.
All inputs are finite; a program needn't handle non-finite values.
Results may differ from a plain program's by a relative error of at most 0.0051.
Values may be sent and summed in bfloat16 or wider, within the bound.
A program may use at most 128 MiB of HBM per device.

v0:
```python
import math
import jax
import jax.numpy as jnp
from jax import lax
from jax.sharding import PartitionSpec as P

ITERS = 2


def residual_block(block, cell_total, frac, limit):
    values = block.astype(jnp.float32)
    expected = cell_total[:, None] * frac[None, :]
    scaled = (values - expected) / jnp.sqrt(expected + 0.01 * expected * expected)
    return jnp.clip(scaled, -limit, limit).astype(jnp.bfloat16)


def self_gram(block):
    return lax.dot_general(
        block,
        block,
        (((0,), (0,)), ((), ())),
        precision=lax.Precision.HIGHEST,
        preferred_element_type=jnp.float32,
    )


def whitening(gram, count):
    width = gram.shape[0]
    identity = jnp.eye(width, dtype=jnp.float32)
    shifted = gram + 1e-05 * jnp.trace(gram) / width * identity
    lower = jnp.linalg.cholesky(shifted)
    inverse = jax.scipy.linalg.solve_triangular(lower, identity, lower=True)
    return jnp.transpose(inverse) * math.sqrt(count)


def transposed_product(left, right):
    return lax.dot_general(
        left, right, (((0,), (0,)), ((), ())), preferred_element_type=jnp.float32
    )


def loading_total(partial_sum, gene_scale):
    return lax.psum(partial_sum, "cells") * gene_scale


def shards(counts, sketch):
    cell_dev, gene_dev = counts.shape
    group_count = lax.axis_size("genes")
    cell_count = float(cell_dev * lax.axis_size("cells"))
    gene_count = float(gene_dev * group_count)
    cell_part = jnp.sum(counts, axis=1).astype(jnp.float32)
    gene_part = jnp.sum(counts, axis=0).astype(jnp.float32)
    gene_total, group_sum = lax.psum((gene_part, jnp.sum(gene_part)), "cells")
    cell_total, grand = lax.psum((cell_part, group_sum), "genes")
    frac = gene_total / grand
    limit = math.sqrt(cell_count)
    resid = residual_block(counts, cell_total, frac, limit)
    gene_scale = math.sqrt(gene_count) / cell_count
    omega = sketch
    basis = None
    loadings = None
    for sweep in range(ITERS):
        sketched = lax.psum(jnp.dot(resid, omega, preferred_element_type=jnp.float32), "genes")
        gram = lax.psum(self_gram(sketched), "cells")
        basis = jnp.dot(sketched, whitening(gram, cell_count), precision=lax.Precision.HIGHEST)
        partial_sum = transposed_product(resid, basis.astype(jnp.bfloat16))
        loadings = loading_total(partial_sum, gene_scale)
        if sweep < ITERS - 1:
            omega = loadings.astype(jnp.bfloat16)
    return (basis, loadings)


def solution(mesh):
    return jax.shard_map(
        shards,
        mesh=mesh,
        in_specs=(P("cells", "genes"), P("genes", None)),
        out_specs=(P("cells", None), P("genes", None)),
        check_vma=False,
    )
```

profile of v0, /device:TPU:0, one launch (start us, length us, event | category | flops | bytes accessed | tf_op | source)
XLA Modules:
  0.0 572.5 jit_solution(13577707791182518231)
XLA Ops:
  7.2 8.2 %fusion.17 = (s32[4864]{0:T(1024)S(1)}, s32[1000]{0:T(1024)S(1)}) fusion(s32[4864,1000]{0,1:T(8,128)} %param.5), kind=kLoop, calls=%fused_computation.43 | loop fusion | flops 9722136 | bytes 19479456 | tf_op jit(solution)/shard_map/reduce_sum | solution.py:51
  16.0 24.0 %all-reduce = (f32[1000]{0:T(1024)S(1)}, f32[]{:T(128)}) all-reduce(f32[1000]{0:T(1024)S(1)} %convert_element_type.29, f32[]{:T(128)} %convert_reduce_fusion), channel_id=1, replica_groups=mesh['cells'=8,'genes'=4] {'cells'}, use_global_device_ids=true, to_apply=%region_3.0 | all-reduce | flops 1001 | bytes 8008 | tf_op jit(solution)/shard_map/psum | solution.py:53
  40.0 11.3 %all-reduce.1 = (f32[]{:T(128)}, f32[4864]{0:T(1024)S(1)}) all-reduce(f32[]{:T(128)} %get-tuple-element.7, f32[4864]{0:T(1024)S(1)} %convert_element_type.28), channel_id=1, replica_groups=mesh['cells'=8,'genes'=4] {'genes'}, use_global_device_ids=true, to_apply=%region_6.0 | all-reduce | flops 4865 | bytes 38920 | tf_op jit(solution)/shard_map/psum | solution.py:54
  51.9 10.2 %fusion.2 = bf16[4864,1000]{0,1:T(8,128)(2,1)S(1)} fusion(s32[4864,1000]{0,1:T(8,128)} %param.5, f32[1000]{0:T(1024)S(1)} %broadcast_divide_fusion, f32[4864]{0:T(1024)S(1)} %get-tuple-element.9), kind=kLoop, calls=%fused_computation.6 | loop fusion | flops 43776000 | bytes 29207456 | tf_op jit(solution)/shard_map/convert_element_type | solution.py:14
  62.1 3.7 copy-done.1
  65.9 4.5 fusion.18
  70.4 54.2 %all-reduce.9.cloned.1.call-done = f32[4864,128]{1,0:T(8,128)} async-done(((f32[4864,128]{1,0:T(8,128)}), f32[4864,128]{1,0:T(8,128)}) %all-reduce.9.cloned.1.call-update) | async-done | bytes 2490384 | tf_op jit(solution)/shard_map/psum | solution.py:63
  124.6 7.3 %fusion.19 = f32[128,128]{0,1:T(8,128)} fusion(f32[4864,128]{1,0:T(8,128)} %all-reduce.9.cloned.1.call-done), kind=kOutput, calls=%fused_computation.45 | convolution fusion | flops 956301312 | bytes 2555904 | tf_op jit(solution)/shard_map/dot_general | solution.py:18
  132.4 69.0 %all-reduce.11.cloned.1.call-done = f32[128,128]{0,1:T(8,128)} async-done(((f32[128,128]{0,1:T(8,128)}), f32[128,128]{0,1:T(8,128)}) %all-reduce.11.cloned.1.call-update) | async-done | bytes 65552 | tf_op jit(solution)/shard_map/psum | solution.py:64
  201.4 1.5 select_reduce_fusion.3
  203.5 0.9 select_add_fusion.1
  204.5 0.9 fusion.15
  205.3 11.7 %cholesky.44 = f32[128,128]{1,0:T(8,128)S(1)} custom-call(f32[128,128]{1,0:T(8,128)S(1)} %fusion.15), custom_call_target="Cholesky" | custom-call | tf_op jit(solution)/shard_map/jit(cholesky)/cholesky | solution.py:31
  218.4 9.8 %custom-call.6 = f32[1,128,128]{1,2,0:T(8,128)S(1)} custom-call(f32[1,128,128]{2,1,0:T(8,128)S(1)} %fusion.10), custom_call_target="InvertDiagBlocksLowerTriangular" | custom-call | tf_op jit(solution)/shard_map/jit(_solve_triangular)/triangular_solve | solution.py:32
  228.5 2.1 convolution_convert_fusion
  230.6 7.3 %fusion.20 = f32[1000,128]{1,0:T(8,128)} fusion(bf16[4864,1000]{0,1:T(8,128)(2,1)} %copy-done.1, bf16[4864,128]{1,0:T(8,128)(2,1)S(1)} %convolution_convert_fusion), kind=kOutput, calls=%fused_computation.46 | convolution fusion | flops 1245184000 | bytes 11485184 | tf_op jit(solution)/shard_map/dot_general | solution.py:37
  238.2 72.4 %all-reduce.13.cloned.1.call-done = f32[1000,128]{1,0:T(8,128)} async-done(((f32[1000,128]{1,0:T(8,128)}), f32[1000,128]{1,0:T(8,128)}) %all-reduce.13.cloned.1.call-update) | async-done | bytes 512016 | tf_op jit(solution)/shard_map/psum | solution.py:43
  310.6 8.1 %fusion.6 = f32[4864,128]{1,0:T(8,128)} fusion(bf16[4864,1000]{0,1:T(8,128)(2,1)} %copy-done.1, f32[1000,128]{1,0:T(8,128)} %all-reduce.13.cloned.1.call-done), kind=kOutput, calls=%fused_computation.14 | convolution fusion | flops 1245440000 | bytes 12730368 | tf_op jit(solution)/shard_map/dot_general | solution.py:63
  318.8 57.2 %all-reduce.15.cloned.1.call-done = f32[4864,128]{1,0:T(8,128)} async-done(((f32[4864,128]{1,0:T(8,128)}), f32[4864,128]{1,0:T(8,128)}) %all-reduce.15.cloned.1.call-update) | async-done | bytes 2490384 | tf_op jit(solution)/shard_map/psum | solution.py:63
  375.9 7.3 %fusion.21 = f32[128,128]{0,1:T(8,128)} fusion(f32[4864,128]{1,0:T(8,128)} %all-reduce.15.cloned.1.call-done), kind=kOutput, calls=%fused_computation.47 | convolution fusion | flops 956301312 | bytes 2555904 | tf_op jit(solution)/shard_map/dot_general | solution.py:18
  383.5 69.2 %all-reduce.17.cloned.1.call-done = f32[128,128]{0,1:T(8,128)} async-done(((f32[128,128]{0,1:T(8,128)}), f32[128,128]{0,1:T(8,128)}) %all-reduce.17.cloned.1.call-update) | async-done | bytes 65552 | tf_op jit(solution)/shard_map/psum | solution.py:64
  452.8 1.5 select_reduce_fusion.2
  454.9 0.9 select_add_fusion
  455.8 0.9 fusion.13
  456.7 11.7 %cholesky.55 = f32[128,128]{1,0:T(8,128)S(1)} custom-call(f32[128,128]{1,0:T(8,128)S(1)} %fusion.13), custom_call_target="Cholesky" | custom-call | tf_op jit(solution)/shard_map/jit(cholesky)/cholesky | solution.py:31
  469.1 0.7 fusion.11
  469.8 9.8 %custom-call.7 = f32[1,128,128]{1,2,0:T(8,128)S(1)} custom-call(f32[1,128,128]{2,1,0:T(8,128)S(1)} %fusion.11), custom_call_target="InvertDiagBlocksLowerTriangular" | custom-call | tf_op jit(solution)/shard_map/jit(_solve_triangular)/triangular_solve | solution.py:32
  479.9 2.2 fusion.22
  482.1 1.4 copy-done.4
  483.5 7.3 %fusion.4 = f32[1000,128]{1,0:T(8,128)} fusion(bf16[4864,1000]{0,1:T(8,128)(2,1)} %copy-done.1, f32[4864,128]{1,0:T(8,128)S(1)} %fusion.22), kind=kOutput, calls=%fused_computation.9 | convolution fusion | flops 1245806592 | bytes 12730368 | tf_op jit(solution)/shard_map/dot_general | solution.py:37
  490.8 72.7 %all-reduce.19.cloned.1.call-done = f32[1000,128]{1,0:T(8,128)} async-done(((f32[1000,128]{1,0:T(8,128)}), f32[1000,128]{1,0:T(8,128)}) %all-reduce.19.cloned.1.call-update) | async-done | bytes 512016 | tf_op jit(solution)/shard_map/psum | solution.py:43
  563.5 1.9 broadcast_multiply_fusion
  (33 shorter events, 5.2 us)
Async XLA Ops:
  7.2 58.7 %copy-start = (bf16[1000,128]{1,0:T(8,128)(2,1)S(1)}, bf16[1000,128]{1,0:T(8,128)(2,1)}, u32[]{:S(2)}) copy-start(bf16[1000,128]{1,0:T(8,128)(2,1)} %param.6) | copy-start | bytes 768004
  7.2 117.4 %all-reduce.9.cloned.1.call-start = ((), (), s32[]{:S(2)}) async-start(), calls=%async_computation | async-start | bytes 4980736 | tf_op jit(solution)/shard_map/psum | solution.py:63
  62.1 3.7 copy-start.1
  70.4 131.0 %all-reduce.11.cloned.1.call-start = ((), (), s32[]{:S(2)}) async-start(), calls=%async_computation.1 | async-start | bytes 131072 | tf_op jit(solution)/shard_map/psum | solution.py:64
  124.6 103.9 %copy-start.3 = (f32[4864,128]{1,0:T(8,128)S(1)}, f32[4864,128]{1,0:T(8,128)}, u32[]{:S(2)}) copy-start(f32[4864,128]{1,0:T(8,128)} %all-reduce.9.cloned.1.call-done) | copy-start | bytes 7471108
  131.9 178.7 %all-reduce.13.cloned.1.call-start = ((), (), s32[]{:S(2)}) async-start(), calls=%async_computation.2 | async-start | bytes 1024000 | tf_op jit(solution)/shard_map/psum | solution.py:43
  237.9 138.0 %all-reduce.15.cloned.1.call-start = ((), (), s32[]{:S(2)}) async-start(), calls=%async_computation.3 | async-start | bytes 4980736 | tf_op jit(solution)/shard_map/psum | solution.py:63
  318.7 134.0 %all-reduce.17.cloned.1.call-start = ((), (), s32[]{:S(2)}) async-start(), calls=%async_computation.4 | async-start | bytes 131072 | tf_op jit(solution)/shard_map/psum | solution.py:64
  375.9 103.9 %copy-start.2 = (f32[4864,128]{1,0:T(8,128)S(1)}, f32[4864,128]{1,0:T(8,128)}, u32[]{:S(2)}) copy-start(f32[4864,128]{1,0:T(8,128)} %all-reduce.15.cloned.1.call-done) | copy-start | bytes 7471108
  383.3 180.2 %all-reduce.19.cloned.1.call-start = ((), (), s32[]{:S(2)}) async-start(), calls=%async_computation.5 | async-start | bytes 1024000 | tf_op jit(solution)/shard_map/psum | solution.py:43
  482.1 1.5 copy-start.4
Sparse Core Ops, SparseCore 0:
  70.5 54.0 all-reduce.8
  132.0 69.3 all-reduce.10
  238.0 72.4 all-reduce.12
  318.9 57.0 all-reduce.14
  383.4 69.3 all-reduce.16
  491.0 72.5 all-reduce.18
where the time goes:
time: 581 us; the launch traced here: 572 us
  waiting for transfers between devices  395 us (68%)
  other arithmetic  73.6 us (13%)
  matrix products  46.6 us (8%)
  blocking collectives  35.3 us (6%)
  between operations  15.8 us (3%)
    psum x2, waiting for transfers between devices, loading_total(): return lax.psum(partial_sum, 'cells') * gene_scale  145 us
    psum x2, waiting for transfers between devices, shards(): gram = lax.psum(self_gram(sketched), 'cells')  138 us
    psum x2, waiting for transfers between devices, shards(): lax.psum(jnp.dot(resid, omega, preferred_element_type=jnp.float32), 'genes')  111 us
    another operation x6, other arithmetic, whitening(): lower = jnp.linalg.cholesky(shifted)  24.8 us
    psum x1, blocking collectives, shards(): gene_total, group_sum = lax.psum((gene_part, jnp.sum(gene_part)), 'cells')  24 us
    another operation x4, other arithmetic, whitening(): inverse = jax.scipy.linalg.solve_triangular(lower, identity, lower=True)  20.9 us
    dot_general x2, matrix products, self_gram(): lax.dot_general(block, block, (((0,), (0,)), ((), ())), precision=lax.Pre...  14.6 us
    dot_general x2, matrix products, transposed_product(): lax.dot_general(left, right, (((0,), (0,)), ((), ())), preferred_element_...  14.6 us
  transfers between devices with their start and end apart: 6, of which 6 were waited for; matrix products, arithmetic and copies ran while one was open for 0% of the time, Pallas kernels for 0%

commit v1 on v0

--- a/solution.py
+++ b/solution.py
@@ -61,7 +61,7 @@
     loadings = None
     for sweep in range(ITERS):
         sketched = lax.psum(jnp.dot(resid, omega, preferred_element_type=jnp.float32), "genes")
-        gram = lax.psum(self_gram(sketched), "cells")
+        gram = lax.all_gather(self_gram(sketched), "cells").sum(axis=0)
         basis = jnp.dot(sketched, whitening(gram, cell_count), precision=lax.Precision.HIGHEST)
         partial_sum = transposed_product(resid, basis.astype(jnp.bfloat16))
         loadings = loading_total(partial_sum, gene_scale)

time: 581 us -> 499 us (0.86)
  waiting for transfers between devices: 395 us -> 256 us
  blocking collectives: 35.3 us -> 99.3 us
    psum x2 -> x0, waiting for transfers between devices: 138 us -> none  [shards(): gram = lax.psum(self_gram(sketched), 'cells')]
    all_gather x0 -> x2, blocking collectives: none -> 64 us  [shards(): gram = lax.all_gather(self_gram(sketched), 'cells').sum(axis=0)]
  transfers between devices with their start and end apart: 6 -> 4, of which waited for: 6 -> 4; matrix products, arithmetic and copies ran while one was open for 0% -> 0% of each run, Pallas kernels for 0% -> 0%
where the time goes in v1:
time: 499 us; the launch traced here: 491 us
  waiting for transfers between devices  256 us (51%)
  blocking collectives  99.3 us (20%)
  other arithmetic  68.6 us (14%)
  matrix products  45.3 us (9%)
  between operations  15.5 us (3%)
  local copies, waits for them, and re-layouts  5.54 us (1%)
    psum x2, waiting for transfers between devices, loading_total(): return lax.psum(partial_sum, 'cells') * gene_scale  145 us
    psum x2, waiting for transfers between devices, shards(): lax.psum(jnp.dot(resid, omega, preferred_element_type=jnp.float32), 'genes')  111 us
    all_gather x2, blocking collectives, shards(): gram = lax.all_gather(self_gram(sketched), 'cells').sum(axis=0)  64 us
    another operation x6, other arithmetic, whitening(): lower = jnp.linalg.cholesky(shifted)  24.8 us
    psum x1, blocking collectives, shards(): gene_total, group_sum = lax.psum((gene_part, jnp.sum(gene_part)), 'cells')  24 us
    another operation x4, other arithmetic, whitening(): inverse = jax.scipy.linalg.solve_triangular(lower, identity, lower=True)  20.9 us
    dot_general x2, matrix products, transposed_product(): lax.dot_general(left, right, (((0,), (0,)), ((), ())), preferred_element_...  14.6 us
    dot_general x2, matrix products, self_gram(): lax.dot_general(block, block, (((0,), (0,)), ((), ())), precision=lax.Pre...  13.3 us
  transfers between devices with their start and end apart: 4, of which 4 were waited for; matrix products, arithmetic and copies ran while one was open for 0% of the time, Pallas kernels for 0%

profile of v1, /device:TPU:0, one launch (start us, length us, event | category | flops | bytes accessed | tf_op | source)
XLA Modules:
  0.0 491.0 jit_solution(16428461358649345848)
XLA Ops:
  7.2 8.2 %fusion.17 = (s32[4864]{0:T(1024)S(1)}, s32[1000]{0:T(1024)S(1)}) fusion(s32[4864,1000]{0,1:T(8,128)} %param.5), kind=kLoop, calls=%fused_computation.43 | loop fusion | flops 9722136 | bytes 19479456 | tf_op jit(solution)/shard_map/reduce_sum | solution.py:51
  16.0 24.0 %all-reduce = (f32[1000]{0:T(1024)S(1)}, f32[]{:T(128)}) all-reduce(f32[1000]{0:T(1024)S(1)} %convert_element_type.29, f32[]{:T(128)} %convert_reduce_fusion), channel_id=1, replica_groups=mesh['cells'=8,'genes'=4] {'cells'}, use_global_device_ids=true, to_apply=%region_3.0 | all-reduce | flops 1001 | bytes 8008 | tf_op jit(solution)/shard_map/psum | solution.py:53
  40.0 11.3 %all-reduce.1 = (f32[]{:T(128)}, f32[4864]{0:T(1024)S(1)}) all-reduce(f32[]{:T(128)} %get-tuple-element.7, f32[4864]{0:T(1024)S(1)} %convert_element_type.28), channel_id=1, replica_groups=mesh['cells'=8,'genes'=4] {'genes'}, use_global_device_ids=true, to_apply=%region_6.0 | all-reduce | flops 4865 | bytes 38920 | tf_op jit(solution)/shard_map/psum | solution.py:54
  51.3 0.6 broadcast_divide_fusion
  51.9 10.2 %fusion.2 = bf16[4864,1000]{0,1:T(8,128)(2,1)S(1)} fusion(s32[4864,1000]{0,1:T(8,128)} %param.5, f32[1000]{0:T(1024)S(1)} %broadcast_divide_fusion, f32[4864]{0:T(1024)S(1)} %get-tuple-element.9), kind=kLoop, calls=%fused_computation.6 | loop fusion | flops 43776000 | bytes 29207456 | tf_op jit(solution)/shard_map/convert_element_type | solution.py:14
  62.1 3.7 copy-done.1
  65.9 4.5 fusion.18
  70.4 54.2 %all-reduce.7.cloned.1.call-done = f32[4864,128]{1,0:T(8,128)} async-done(((f32[4864,128]{1,0:T(8,128)}), f32[4864,128]{1,0:T(8,128)}) %all-reduce.7.cloned.1.call-update) | async-done | bytes 2490384 | tf_op jit(solution)/shard_map/psum | solution.py:63
  124.6 6.7 %fusion.19 = f32[128,128]{1,0:T(8,128)S(1)} fusion(f32[4864,128]{1,0:T(8,128)} %all-reduce.7.cloned.1.call-done), kind=kOutput, calls=%fused_computation.45 | convolution fusion | flops 956301312 | bytes 2555904 | tf_op jit(solution)/shard_map/dot_general | solution.py:18
  131.2 32.1 %all-gather = f32[1024,128]{1,0:T(8,128)S(1)} all-gather(f32[128,128]{1,0:T(8,128)S(1)} %fusion.19), channel_id=2, replica_groups=mesh['cells'=8,'genes'=4] {'cells'}, dimensions={0}, use_global_device_ids=true | all-gather | bytes 589824 | tf_op jit(solution)/shard_map/all_gather | solution.py:64
  163.5 0.6 select_reduce_fusion.3
  164.9 11.7 %cholesky.44 = f32[128,128]{1,0:T(8,128)S(1)} custom-call(f32[128,128]{1,0:T(8,128)S(1)} %fusion.15), custom_call_target="Cholesky" | custom-call | tf_op jit(solution)/shard_map/jit(cholesky)/cholesky | solution.py:31
  176.7 0.6 compare_reduce_fusion.1
  177.3 0.7 fusion.10
  178.0 9.8 %custom-call.6 = f32[1,128,128]{1,2,0:T(8,128)S(1)} custom-call(f32[1,128,128]{2,1,0:T(8,128)S(1)} %fusion.10), custom_call_target="InvertDiagBlocksLowerTriangular" | custom-call | tf_op jit(solution)/shard_map/jit(_solve_triangular)/triangular_solve | solution.py:32
  188.1 2.1 convolution_convert_fusion
  190.2 7.3 %fusion.20 = f32[1000,128]{1,0:T(8,128)} fusion(bf16[4864,1000]{0,1:T(8,128)(2,1)} %copy-done.1, bf16[4864,128]{1,0:T(8,128)(2,1)S(1)} %convolution_convert_fusion), kind=kOutput, calls=%fused_computation.46 | convolution fusion | flops 1245184000 | bytes 11485184 | tf_op jit(solution)/shard_map/dot_general | solution.py:37
  197.7 72.4 %all-reduce.9.cloned.1.call-done = f32[1000,128]{1,0:T(8,128)} async-done(((f32[1000,128]{1,0:T(8,128)}), f32[1000,128]{1,0:T(8,128)}) %all-reduce.9.cloned.1.call-update) | async-done | bytes 512016 | tf_op jit(solution)/shard_map/psum | solution.py:43
  270.1 8.1 %fusion.6 = f32[4864,128]{1,0:T(8,128)} fusion(bf16[4864,1000]{0,1:T(8,128)(2,1)} %copy-done.1, f32[1000,128]{1,0:T(8,128)} %all-reduce.9.cloned.1.call-done), kind=kOutput, calls=%fused_computation.14 | convolution fusion | flops 1245440000 | bytes 12730368 | tf_op jit(solution)/shard_map/dot_general | solution.py:63
  278.3 57.2 %all-reduce.11.cloned.1.call-done = f32[4864,128]{1,0:T(8,128)} async-done(((f32[4864,128]{1,0:T(8,128)}), f32[4864,128]{1,0:T(8,128)}) %all-reduce.11.cloned.1.call-update) | async-done | bytes 2490384 | tf_op jit(solution)/shard_map/psum | solution.py:63
  335.5 6.7 %fusion.21 = f32[128,128]{1,0:T(8,128)S(1)} fusion(f32[4864,128]{1,0:T(8,128)} %all-reduce.11.cloned.1.call-done), kind=kOutput, calls=%fused_computation.47 | convolution fusion | flops 956301312 | bytes 2555904 | tf_op jit(solution)/shard_map/dot_general | solution.py:18
  342.2 31.9 %all-gather.1 = f32[1024,128]{1,0:T(8,128)S(1)} all-gather(f32[128,128]{1,0:T(8,128)S(1)} %fusion.21), channel_id=3, replica_groups=mesh['cells'=8,'genes'=4] {'cells'}, dimensions={0}, use_global_device_ids=true | all-gather | bytes 589824 | tf_op jit(solution)/shard_map/all_gather | solution.py:64
  374.2 0.6 select_reduce_fusion.2
  375.6 11.7 %cholesky.55 = f32[128,128]{1,0:T(8,128)S(1)} custom-call(f32[128,128]{1,0:T(8,128)S(1)} %fusion.13), custom_call_target="Cholesky" | custom-call | tf_op jit(solution)/shard_map/jit(cholesky)/cholesky | solution.py:31
  387.3 0.6 compare_reduce_fusion
  388.0 0.7 fusion.11
  388.6 9.8 %custom-call.7 = f32[1,128,128]{1,2,0:T(8,128)S(1)} custom-call(f32[1,128,128]{2,1,0:T(8,128)S(1)} %fusion.11), custom_call_target="InvertDiagBlocksLowerTriangular" | custom-call | tf_op jit(solution)/shard_map/jit(_solve_triangular)/triangular_solve | solution.py:32
  398.8 2.2 fusion.22
  401.0 1.4 copy-done.4
  402.4 7.3 %fusion.4 = f32[1000,128]{1,0:T(8,128)} fusion(bf16[4864,1000]{0,1:T(8,128)(2,1)} %copy-done.1, f32[4864,128]{1,0:T(8,128)S(1)} %fusion.22), kind=kOutput, calls=%fused_computation.9 | convolution fusion | flops 1245806592 | bytes 12730368 | tf_op jit(solution)/shard_map/dot_general | solution.py:37
  409.7 72.7 %all-reduce.13.cloned.1.call-done = f32[1000,128]{1,0:T(8,128)} async-done(((f32[1000,128]{1,0:T(8,128)}), f32[1000,128]{1,0:T(8,128)}) %all-reduce.13.cloned.1.call-update) | async-done | bytes 512016 | tf_op jit(solution)/shard_map/psum | solution.py:43
  482.4 1.9 broadcast_multiply_fusion
  (33 shorter events, 2.2 us)
Async XLA Ops:
  7.2 58.7 %copy-start = (bf16[1000,128]{1,0:T(8,128)(2,1)S(1)}, bf16[1000,128]{1,0:T(8,128)(2,1)}, u32[]{:S(2)}) copy-start(bf16[1000,128]{1,0:T(8,128)(2,1)} %param.6) | copy-start | bytes 768004
  7.2 117.4 %all-reduce.7.cloned.1.call-start = ((), (), s32[]{:S(2)}) async-start(), calls=%async_computation | async-start | bytes 4980736 | tf_op jit(solution)/shard_map/psum | solution.py:63
  62.1 3.7 copy-start.1
  70.4 199.8 %all-reduce.9.cloned.1.call-start = ((), (), s32[]{:S(2)}) async-start(), calls=%async_computation.1 | async-start | bytes 1024000 | tf_op jit(solution)/shard_map/psum | solution.py:43
  124.6 63.5 %copy-start.3 = (f32[4864,128]{1,0:T(8,128)S(1)}, f32[4864,128]{1,0:T(8,128)}, u32[]{:S(2)}) copy-start(f32[4864,128]{1,0:T(8,128)} %all-reduce.7.cloned.1.call-done) | copy-start | bytes 7471108
  197.5 138.0 %all-reduce.11.cloned.1.call-start = ((), (), s32[]{:S(2)}) async-start(), calls=%async_computation.2 | async-start | bytes 4980736 | tf_op jit(solution)/shard_map/psum | solution.py:63
  278.3 204.1 %all-reduce.13.cloned.1.call-start = ((), (), s32[]{:S(2)}) async-start(), calls=%async_computation.3 | async-start | bytes 1024000 | tf_op jit(solution)/shard_map/psum | solution.py:43
  335.5 63.3 %copy-start.2 = (f32[4864,128]{1,0:T(8,128)S(1)}, f32[4864,128]{1,0:T(8,128)}, u32[]{:S(2)}) copy-start(f32[4864,128]{1,0:T(8,128)} %all-reduce.11.cloned.1.call-done) | copy-start | bytes 7471108
  400.9 1.5 copy-start.4
Sparse Core Ops, SparseCore 0:
  70.5 54.0 all-reduce.6
  197.6 72.4 all-reduce.8
  278.4 57.0 all-reduce.10
  409.8 72.5 all-reduce.12
